TPU v7x, 32 devices: a whole 2x2x4 slice. The times are simulated.
32 devices in a mesh: groups: 2 (over y), expert: 8 (over z, x), tensor: 2 (over core).
Axes of the slice: x: 2, y: 2, z: 4, core: 2. Of those that a mesh axis runs over, the one named last changes fastest.
Arguments:
- tokens: bfloat16 [4096, 1440], P(('groups', 'expert')), parts along dimension 0, may hold values from -6 to 6
- routes: int32 [4096, 4], P(('groups', 'expert')), parts along dimension 0, may hold values from 0 to 7, all different within a row; in each aligned block of 256 rows (0 to 255, 256 to 511, ...) at most 192 rows name the same one
- gates: float32 [4096, 4], P(('groups', 'expert')), parts along dimension 0, may hold values from 0.1 to 1
- w_gate: bfloat16 [8, 1440, 1440], P('expert', None, 'tensor'), may hold values from -0.15625 to 0.15625
- w_up: bfloat16 [8, 1440, 1440], P('expert', None, 'tensor'), may hold values from -0.15625 to 0.15625
- w_down: bfloat16 [8, 1440, 1440], P('expert', 'tensor'), may hold values from -0.15625 to 0.15625
- shared_gate: bfloat16 [1440, 1440], P(None, 'tensor'), may hold values from -0.15625 to 0.15625
- shared_up: bfloat16 [1440, 1440], P(None, 'tensor'), may hold values from -0.15625 to 0.15625
- shared_down: bfloat16 [1440, 1440], P('tensor'), may hold values from -0.15625 to 0.15625
Outputs:
- mixed: bfloat16 [4096, 1440], P(('groups', 'expert'), 'tensor'), parts along dimension 0
There are 2 independent parts, one for each index of `groups`. A program takes and returns all parts, laid end to end along the dimension named above; an argument that names none is the same for every part. Nothing has to cross between parts.
Inputs may be any that keep to these rules, and one draw needn't show every extreme that they name: `routes`: each token names 4 different experts. Among the 256 tokens of one index of expert (aligned blocks of rows), no expert is named by more than 192 tokens; in some blocks one expert is named by exactly 192.
All inputs are finite; a program needn't handle non-finite values.
Results may differ from a plain program's by a relative error of at most 0.0051.
Values may be sent and summed in bfloat16 or wider, within the bound.
A program may use at most 192 MiB of HBM per device.

v0:
```python
import jax
import jax.numpy as jnp
from jax import lax
from jax.sharding import PartitionSpec as P


def local(tokens, routes, gates, w_gate, w_up, w_down, shared_gate, shared_up, shared_down):
    tok_count, top_count = routes.shape
    width_all = tokens.shape[1]
    local_experts = w_gate.shape[0]
    expert_count = lax.axis_size("expert")
    experts_all = expert_count * local_experts
    capacity = max(2, (3 * tok_count * top_count + 2 * experts_all - 1) // (2 * experts_all))
    flat_routes = routes.reshape(-1)
    onehot = (flat_routes[:, None] == jnp.arange(experts_all, dtype=jnp.int32)[None, :]).astype(
        jnp.int32
    )
    order_in = jnp.sum(jnp.cumsum(onehot, axis=0) * onehot, axis=1) - 1
    slot_index = flat_routes * capacity + order_in
    half_width = width_all // lax.axis_size("tensor")
    own_cols = lax.dynamic_slice_in_dim(
        tokens, lax.axis_index("tensor") * half_width, half_width, 1
    )
    outgoing = jnp.zeros((experts_all * capacity, half_width), jnp.bfloat16)
    outgoing = outgoing.at[slot_index].set(jnp.repeat(own_cols, top_count, axis=0))
    outgoing = outgoing.reshape(experts_all, capacity, half_width)
    received = lax.all_to_all(outgoing, "expert", split_axis=0, concat_axis=0, tiled=True)
    received = lax.all_gather(received, "tensor", axis=2, tiled=True)
    item_rows = received.shape[1]
    stacked = received.reshape(expert_count, local_experts, item_rows, width_all)
    stacked = stacked.transpose(1, 0, 2, 3).reshape(
        local_experts, expert_count * item_rows, width_all
    )
    gate_val = jnp.einsum("emd,edf->emf", stacked, w_gate, preferred_element_type=jnp.float32)
    up_val = jnp.einsum("emd,edf->emf", stacked, w_up, preferred_element_type=jnp.float32)
    hidden = (jax.nn.silu(gate_val) * up_val).astype(jnp.bfloat16)
    partial_value = jnp.einsum("emf,efd->emd", hidden, w_down, preferred_element_type=jnp.float32)
    partial_value = partial_value.reshape(local_experts, expert_count, item_rows, width_all)
    partial_value = partial_value.transpose(1, 0, 2, 3).reshape(experts_all, item_rows, width_all)
    summed = lax.psum_scatter(partial_value, "tensor", scatter_dimension=2, tiled=True).astype(
        jnp.bfloat16
    )
    returned = lax.all_to_all(summed, "expert", split_axis=0, concat_axis=0, tiled=True)
    shared_g = jnp.dot(tokens, shared_gate, preferred_element_type=jnp.float32)
    shared_u = jnp.dot(tokens, shared_up, preferred_element_type=jnp.float32)
    shared_hidden = (jax.nn.silu(shared_g) * shared_u).astype(jnp.bfloat16)
    shared_part = jnp.dot(shared_hidden, shared_down, preferred_element_type=jnp.float32)
    picked = returned.reshape(experts_all * capacity, half_width)[slot_index]
    picked = picked.astype(jnp.float32).reshape(tok_count, top_count, half_width)
    routed = jnp.sum(gates[:, :, None] * picked, axis=1)
    total = routed + lax.psum_scatter(shared_part, "tensor", scatter_dimension=1, tiled=True)
    return (own_cols.astype(jnp.float32) + total).astype(jnp.bfloat16)


def solution(mesh):
    in_specs = (
        P(("groups", "expert"), None),
        P(("groups", "expert"), None),
        P(("groups", "expert"), None),
        P("expert", None, "tensor"),
        P("expert", None, "tensor"),
        P("expert", "tensor", None),
        P(None, "tensor"),
        P(None, "tensor"),
        P("tensor", None),
    )
    out_specs = P(("groups", "expert"), "tensor")
    return jax.shard_map(local, mesh=mesh, in_specs=in_specs, out_specs=out_specs, check_vma=False)
```

profile of v0, /device:TPU:1, one launch (start us, length us, event | category | flops | bytes accessed | tf_op | source)
XLA Modules:
  0.0 273.9 jit_solution(7017293416012651692)
XLA Ops:
  6.5 0.0 copy-start
  6.5 0.0 all-gather.2.cloned.1.call-start
  6.5 1.0 copy.28
  7.5 0.1 eq.29
  7.6 0.1 eq.25
  7.8 0.7 broadcast_multiply_fusion
  8.4 1.0 constant_dynamic-slice_fusion
  9.5 0.2 copy.30
  9.6 1.6 broadcast_in_dim.5
  11.2 3.7 %reshape.116 = bf16[1024,720]{1,0:T(8,128)(2,1)} reshape(bf16[256,4,720]{2,1,0:T(4,128)(2,1)} %broadcast_in_dim.5) | data formatting | bytes 2949120 | tf_op jit(solution)/shard_map/reshape | solution.py:25
  14.9 2.3 reduce-window.6
  17.2 0.3 slice_reduce_fusion
  17.5 0.2 reduce-window.9
  17.6 0.1 add_bitcast_fusion
  17.8 0.1 copy.27
  17.9 0.1 mul.50
  18.0 7.5 %scatter_custom_fusion = bf16[1536,720]{1,0:T(8,128)(2,1)} fusion(s32[1024]{0:T(1024)S(1)} %bitcast.48, bf16[1024,720]{1,0:T(8,128)(2,1)} %reshape.116, bf16[]{:T(256)} %constant.8.clone.1), kind=kCustom, calls=%fused_computation.11 | custom fusion | bytes 2212352 | tf_op jit(solution)/shard_map/scatter | solution.py:25
  25.5 59.4 %all_to_all.10 = bf16[8,192,720]{2,1,0:T(8,128)(2,1)} all-to-all(bf16[8,192,720]{2,1,0:T(8,128)(2,1)} %bitcast.44), channel_id=1, replica_groups=mesh['groups'=2,'expert'=8,'tensor'=2] {'expert'}, dimensions={0} | all-to-all | bytes 4423680 | tf_op jit(solution)/shard_map/all_to_all | solution.py:27
  84.9 5.1 %copy.31 = bf16[8,192,720]{1,0,2:T(8,128)(2,1)} copy(bf16[8,192,720]{2,1,0:T(8,128)(2,1)} %all_to_all.10) | data formatting | bytes 4423680 | tf_op jit(solution)/shard_map/all_to_all | solution.py:27
  90.0 0.0 all-gather.2.cloned.1.call-update
  90.0 0.2 reduce-scatter.7.cloned.1.call-start
  90.2 16.7 %all-gather.2.cloned.1.call-done = bf16[8,192,1440]{1,0,2:T(8,128)(2,1)} async-done(((bf16[8,192,720]{1,0,2:T(8,128)(2,1)}), bf16[8,192,1440]{1,0,2:T(8,128)(2,1)}) %all-gather.2.cloned.1.call-update) | async-done | bytes 4423696 | tf_op jit(solution)/shard_map/all_gather | solution.py:28
  106.9 8.6 %copy.32 = bf16[8,192,1440]{2,1,0:T(8,128)(2,1)} copy(bf16[8,192,1440]{1,0,2:T(8,128)(2,1)} %all-gather.2.cloned.1.call-done) | data formatting | bytes 8847360 | tf_op jit(solution)/shard_map/all_gather | solution.py:28
  115.5 0.0 copy-start.2
  115.5 0.0 copy-start.5
  115.5 6.5 %fusion.3 = f32[1536,720]{0,1:T(8,128)S(1)} fusion(bf16[1536,1440]{1,0:T(8,128)(2,1)} %bitcast.45, bf16[1,1440,720]{2,1,0:T(8,128)(2,1)} %param.12), kind=kOutput, calls=%fused_computation.7 | convolution fusion | flops 3185049600 | bytes 10920960 | tf_op jit(solution)/shard_map/emd,edf->emf/dot_general | solution.py:34
  122.1 0.0 copy-done.2
  122.1 0.0 copy-done.5
  122.1 5.7 %multiply_convert_fusion = bf16[1536,720]{0,1:T(8,128)(2,1)} fusion(f32[1536,720]{0,1:T(8,128)S(1)} %fusion.3, bf16[1536,1440]{1,0:T(8,128)(2,1)S(1)} %bitcast.46, bf16[1,1440,720]{2,1,0:T(8,128)(2,1)S(1)} %copy-done.5), kind=kOutput, calls=%fused_computation.2 | convolution fusion | flops 3191685120 | bytes 13132800 | tf_op jit(solution)/shard_map/emd,edf->emf/dot_general | solution.py:35
  127.8 4.2 %copy.33 = bf16[1536,720]{1,0:T(8,128)(2,1)} copy(bf16[1536,720]{0,1:T(8,128)(2,1)} %multiply_convert_fusion) | data formatting | bytes 4423680 | tf_op jit(solution)/shard_map/convert_element_type | solution.py:36
  132.0 0.0 copy-done
  132.0 8.0 %fusion = f32[8,192,1440]{2,1,0:T(8,128)} fusion(bf16[8,192,720]{2,1,0:T(8,128)(2,1)} %bitcast.47, bf16[1,720,1440]{2,1,0:T(8,128)(2,1)S(1)} %copy-done), kind=kOutput, calls=%fused_computation.4 | convolution fusion | flops 3185049600 | bytes 13132800 | tf_op jit(solution)/shard_map/emf,efd->emd/dot_general | solution.py:37
  140.0 12.6 %copy.35 = f32[8,192,1440]{1,0,2:T(8,128)} copy(f32[8,192,1440]{2,1,0:T(8,128)} %fusion) | data formatting | bytes 17694720
  152.6 12.4 %reshape.121 = f32[1440,1536]{1,0:T(8,128)} reshape(f32[1440,8,192]{2,1,0:T(8,128)} %bitcast.42) | data formatting | bytes 17694720
  165.0 0.0 reduce-scatter.7.cloned.1.call-update
  165.0 18.2 %reduce-scatter.7.cloned.1.call-done = f32[720,1536]{1,0:T(8,128)} async-done(((f32[1440,1536]{1,0:T(8,128)}), f32[720,1536]{1,0:T(8,128)}) %reduce-scatter.7.cloned.1.call-update) | async-done | bytes 4423696
  183.2 4.7 %reshape.122 = bf16[720,8,192]{2,1,0:T(8,128)(2,1)S(1)} reshape(f32[720,1536]{1,0:T(8,128)} %reduce-scatter.7.cloned.1.call-done) | data formatting | bytes 6635520
  187.9 3.6 %copy.36 = bf16[8,192,720]{2,1,0:T(8,128)(2,1)} copy(bf16[8,192,720]{1,0,2:T(8,128)(2,1)S(1)} %bitcast.43) | data formatting | bytes 4423680
  191.6 0.0 copy-start.3
  191.6 5.6 %all-to-all-start.1 = ((bf16[8,192,720]{2,1,0:T(8,128)(2,1)}), bf16[8,192,720]{2,1,0:T(8,128)(2,1)S(1)}, u32[]{:S(2)}, u32[]{:S(2)}) async-start(bf16[8,192,720]{2,1,0:T(8,128)(2,1)} %copy.36), calls=%async_computation.1 | async-start | bytes 4718592 | tf_op jit(solution)/shard_map/all_to_all | solution.py:43
  197.2 0.3 reduce-scatter.5.cloned.1.call-start
  197.4 0.0 copy-done.3
  197.4 3.5 %fusion.19 = f32[256,720]{0,1:T(8,128)} fusion(bf16[256,1440]{0,1:T(8,128)(2,1)S(1)} %copy-done.3, bf16[1440,720]{1,0:T(8,128)(2,1)} %param.15), kind=kOutput, calls=%fused_computation.35 | convolution fusion | flops 530841600 | bytes 3548160 | tf_op jit(solution)/shard_map/dot_general | solution.py:44
  201.0 0.0 copy-start.4
  201.0 6.2 %fusion.8 = f32[256,1440]{0,1:T(8,128)} fusion(bf16[720,1440]{1,0:T(8,128)(2,1)} %param.17, bf16[256,1440]{0,1:T(8,128)(2,1)S(1)} %copy-done.3, bf16[1440,720]{1,0:T(8,128)(2,1)} %param.16, f32[256,720]{0,1:T(8,128)} %fusion.19), kind=kOutput, calls=%fused_computation.13 | convolution fusion | flops 1062789120 | bytes 7096320 | tf_op jit(solution)/shard_map/dot_general | solution.py:47
  207.1 0.0 reduce-scatter.5.cloned.1.call-update
  207.1 0.0 copy-done.4
  207.2 0.1 copy.26
  207.3 43.2 %all-to-all-done.1 = bf16[8,192,720]{2,1,0:T(8,128)(2,1)S(1)} async-done(((bf16[8,192,720]{2,1,0:T(8,128)(2,1)}), bf16[8,192,720]{2,1,0:T(8,128)(2,1)S(1)}, u32[]{:S(2)}, u32[]{:S(2)}) %all-to-all-start.1) | async-done | bytes 2211872 | tf_op jit(solution)/shard_map/all_to_all | solution.py:43
  250.5 5.2 %gather_fusion = bf16[1024,720]{1,0:T(8,128)(2,1)} fusion(bf16[1536,720]{1,0:T(8,128)(2,1)S(1)} %bitcast.41, s32[1024]{0:T(1024)S(1)} %broadcast_clamp_fusion), kind=kCustom, calls=%fused_computation | custom fusion | bytes 2953216 | tf_op jit(solution)/shard_map/gather | solution.py:48
  255.7 4.2 %reshape.103 = f32[256,4,720]{2,1,0:T(4,128)} reshape(bf16[1024,720]{1,0:T(8,128)(2,1)} %gather_fusion) | data formatting | bytes 4423680 | tf_op jit(solution)/shard_map/convert_element_type | solution.py:49
  260.0 0.0 copy-start.1
  260.0 4.0 %multiply_reduce_fusion = f32[256,720]{1,0:T(8,128)S(1)} fusion(f32[256,4,720]{2,1,0:T(4,128)} %reshape.103, f32[256,4]{1,0:T(8,128)S(1)} %copy.26), kind=kLoop, calls=%fused_computation.3 | loop fusion | flops 1290240 | bytes 3690496 | tf_op jit(solution)/shard_map/reduce_sum | solution.py:50
  264.0 1.1 copy.34
  265.1 0.0 reduce-scatter.5.cloned.1.call-done
  265.1 2.3 add_convert_fusion
  267.4 0.0 copy-done.1
  (5 shorter events, 0.0 us)
Async XLA Ops:
  6.5 125.5 %copy-start = (bf16[1,720,1440]{2,1,0:T(8,128)(2,1)S(1)}, bf16[1,720,1440]{2,1,0:T(8,128)(2,1)}, u32[]{:S(2)}) copy-start(bf16[1,720,1440]{2,1,0:T(8,128)(2,1)} %param.14) | copy-start | bytes 6220804
  6.5 100.4 %all-gather.2.cloned.1.call-start = ((), (), s32[]{:S(2)}) async-start(), calls=%async_computation.4 | async-start | bytes 8847360 | tf_op jit(solution)/shard_map/all_gather | solution.py:28
  90.0 93.2 %reduce-scatter.7.cloned.1.call-start = ((), (), s32[]{:S(2)}) async-start(), calls=%async_computation.6 | async-start | bytes 13271040
  115.5 6.6 %copy-start.2 = (bf16[8,192,1440]{2,1,0:T(8,128)(2,1)S(1)}, bf16[8,192,1440]{2,1,0:T(8,128)(2,1)}, u32[]{:S(2)}) copy-start(bf16[8,192,1440]{2,1,0:T(8,128)(2,1)} %copy.32) | copy-start | bytes 13271044
  115.5 6.6 %copy-start.5 = (bf16[1,1440,720]{2,1,0:T(8,128)(2,1)S(1)}, bf16[1,1440,720]{2,1,0:T(8,128)(2,1)}, u32[]{:S(2)}) copy-start(bf16[1,1440,720]{2,1,0:T(8,128)(2,1)} %param.13) | copy-start | bytes 6220804
  191.6 5.8 %copy-start.3 = (bf16[256,1440]{0,1:T(8,128)(2,1)S(1)}, bf16[256,1440]{0,1:T(8,128)(2,1)}, u32[]{:S(2)}) copy-start(bf16[256,1440]{0,1:T(8,128)(2,1)} %param.9) | copy-start | bytes 2211844
  191.6 58.9 %all-to-all-start.1 = ((bf16[8,192,720]{2,1,0:T(8,128)(2,1)}), bf16[8,192,720]{2,1,0:T(8,128)(2,1)S(1)}, u32[]{:S(2)}, u32[]{:S(2)}) async-start(bf16[8,192,720]{2,1,0:T(8,128)(2,1)} %copy.36), calls=%async_computation.1 | async-start | bytes 4718592 | tf_op jit(solution)/shard_map/all_to_all | solution.py:43
  197.2 68.0 %reduce-scatter.5.cloned.1.call-start = ((), (), s32[]{:S(2)}) async-start(), calls=%async_computation.5 | async-start | bytes 2211840 | tf_op jit(solution)/shard_map/reduce_scatter | solution.py:51
  201.0 6.2 %copy-start.4 = (f32[256,4]{0,1:T(4,128)S(1)}, f32[256,4]{0,1:T(4,128)}, u32[]{:S(2)}) copy-start(f32[256,4]{0,1:T(4,128)} %param.11) | copy-start | bytes 12292
  260.0 7.4 %copy-start.1 = (bf16[1,720,1440]{2,1,0:T(8,128)(2,1)S(1)}, bf16[1,720,1440]{2,1,0:T(8,128)(2,1)}, u32[]{:S(2)}) copy-start(bf16[1,720,1440]{2,1,0:T(8,128)(2,1)} %param.14) | copy-start | bytes 6220804
Sparse Core Ops, SparseCore 0:
  90.1 16.7 all-gather.1
  165.2 17.9 reduce-scatter.6
  207.3 10.4 reduce-scatter.4
where the time goes:
time: 277 us; the launch traced here: 274 us
  waiting for transfers between devices  78.1 us (28%)
  local copies, waits for them, and re-layouts  77.7 us (28%)
  blocking collectives  59.4 us (21%)
  matrix products  29.8 us (11%)
  between operations  13.2 us (5%)
  other arithmetic  9.54 us (3%)
  starting transfers between devices  6.05 us (2%)
    all_to_all x1, blocking collectives, local(): lax.all_to_all(outgoing, 'expert', split_axis=0, concat_axis=0, tiled=True)  59.4 us
    all_to_all x1, waiting for transfers between devices, local(): lax.all_to_all(summed, 'expert', split_axis=0, concat_axis=0, tiled=True)  43.2 us
    unnamed x18, local copies, waits for them, and re-layouts  34.6 us
    unnamed x4, waiting for transfers between devices  18.2 us
    all_gather x1, waiting for transfers between devices, local(): received = lax.all_gather(received, 'tensor', axis=2, tiled=True)  16.7 us
    all_gather x1, local copies, waits for them, and re-layouts, local(): received = lax.all_gather(received, 'tensor', axis=2, tiled=True)  8.61 us
    dot_general x1, matrix products, local(): jnp.einsum('emf,efd->emd', hidden, w_down, preferred_element_type=jnp.flo...  7.96 us
    scatter x1, local copies, waits for them, and re-layouts, local(): outgoing.at[slot_index].set(jnp.repeat(own_cols, top_count, axis=0))  7.47 us
  transfers between devices with their start and end apart: 4, of which 3 were waited for; matrix products, arithmetic and copies ran while one was open for 9% of the time, Pallas kernels for 0%

commit v1 on v0

--- a/solution.py
+++ b/solution.py
@@ -1,10 +1,17 @@
+import functools
+
 import jax
 import jax.numpy as jnp
 from jax import lax
+from jax.experimental import pallas as pl
+from jax.experimental.pallas import tpu as pltpu
 from jax.sharding import PartitionSpec as P
 
-
-def local(tokens, routes, gates, w_gate, w_up, w_down, shared_gate, shared_up, shared_down):
+MESH = pl.DeviceIdType.MESH
+VMEM_BUDGET = 52 * 1024 * 1024
+
+
+def exchange_local(tokens, routes, gates, w_gate, w_up, w_down, shared_gate, shared_up, shared_down):
     tok_count, top_count = routes.shape
     width_all = tokens.shape[1]
     local_experts = w_gate.shape[0]
@@ -50,6 +57,264 @@
     routed = jnp.sum(gates[:, :, None] * picked, axis=1)
     total = routed + lax.psum_scatter(shared_part, "tensor", scatter_dimension=1, tiled=True)
     return (own_cols.astype(jnp.float32) + total).astype(jnp.bfloat16)
+
+
+def silu_mul(g, u):
+    return (g / (1.0 + jnp.exp(-g)) * u).astype(jnp.bfloat16)
+
+
+def moe_kernel(nz, nx, width, ext_ref, tok_ref, wg_ref, wu_ref, wd_ref, sg_ref, su_ref, sd_ref, out_ref,
+               X, Wg, Wu, Wd, Sg, Su, Sd, OWN, O, PXs, PXr, CSs, CSr, SHo, SHs, SHr, FXs, FXr,
+               w_loc, s_loc, w_send, w_recv, z_send, z_recv, x_send, x_recv, p_send, p_recv,
+               c_send, c_recv, m_send, m_recv):
+    me = lax.axis_index("expert")
+    core = lax.axis_index("tensor")
+    z = me // nx
+    x = me % nx
+    ox = nx - 1 - x
+    other = z * nx + ox
+    rows = ext_ref.shape[0]
+    half = out_ref.shape[1]
+
+    barrier = pltpu.get_barrier_semaphore()
+    for d in range(1, nz):
+        peer = ((z + d) % nz) * nx + x
+        pl.semaphore_signal(barrier, inc=1, device_id={"expert": peer}, device_id_type=MESH)
+    pl.semaphore_signal(barrier, inc=1, device_id={"expert": other}, device_id_type=MESH)
+    pl.semaphore_signal(barrier, inc=1, device_id={"tensor": 1 - core}, device_id_type=MESH)
+
+    loc_s = [pltpu.make_async_copy(a, b, s_loc.at[i]) for i, (a, b) in enumerate(
+        ((sg_ref, Sg), (su_ref, Su), (sd_ref, Sd)))]
+    loc_w = [pltpu.make_async_copy(a.at[0], b.at[0], w_loc.at[i]) for i, (a, b) in enumerate(
+        ((wg_ref, Wg), (wu_ref, Wu), (wd_ref, Wd)))]
+    for cp in loc_s + loc_w:
+        cp.start()
+    X[me] = ext_ref[...]
+    pl.semaphore_wait(barrier, nz + 1)
+
+    def remote(src, dst, ssem, rsem, **dev):
+        return pltpu.make_async_remote_copy(src_ref=src, dst_ref=dst, send_sem=ssem, recv_sem=rsem,
+                                            device_id=dev, device_id_type=MESH)
+
+    def z_copy(zo, side):
+        e = zo * nx + x
+        peer = me + nx if side == 0 else me - nx
+        return remote(X.at[e], X.at[e], z_send.at[side, zo], z_recv.at[zo], expert=peer)
+
+    def x_copy(zo, col):
+        e = zo * nx + col
+        return remote(X.at[e], X.at[e], x_send.at[zo], x_recv.at[zo], expert=other)
+
+    def forward(zo):
+        @pl.when(jnp.logical_and(zo <= z, z + 1 < nz))
+        def _():
+            z_copy(zo, 0).start()
+
+        @pl.when(jnp.logical_and(zo >= z, z >= 1))
+        def _():
+            z_copy(zo, 1).start()
+
+        x_copy(zo, x).start()
+
+    def p_copy(zo):
+        return remote(PXs.at[zo], PXr.at[zo], p_send.at[zo], p_recv.at[zo], expert=other)
+
+    def c_copy(zo, slot):
+        return remote(CSs.at[zo], CSr.at[slot], c_send.at[zo], c_recv.at[slot], expert=zo * nx + x)
+
+    forward(z)
+    rem_w = [remote(a.at[0], b.at[1], w_send.at[i], w_recv.at[i], tensor=1 - core) for i, (a, b) in enumerate(
+        ((wg_ref, Wg), (wu_ref, Wu), (wd_ref, Wd)))]
+    for cp in rem_w:
+        cp.start()
+
+    table = [sorted(range(nz), key=lambda q: (abs(q - k), q)) for k in range(nz)]
+
+    def nth(i):
+        r = table[0][i]
+        for k in range(1, nz):
+            r = jnp.where(z == k, table[k][i], r)
+        return r
+
+    for cp in loc_s:
+        cp.wait()
+    tok = tok_ref[...]
+    sh = silu_mul(jnp.dot(tok, Sg[...], preferred_element_type=jnp.float32),
+                  jnp.dot(tok, Su[...], preferred_element_type=jnp.float32))
+    SHo[...] = jnp.dot(sh, Sd[...], preferred_element_type=jnp.float32)
+
+    @pl.when(core == 0)
+    def _():
+        SHs[...] = SHo[:, half:]
+
+    @pl.when(core == 1)
+    def _():
+        SHs[...] = SHo[:, :half]
+    sh_copy = remote(SHs, SHr, m_send.at[0], m_recv.at[0], tensor=1 - core)
+    sh_copy.start()
+
+    for cp in loc_w:
+        cp.wait()
+    for cp in rem_w:
+        cp.wait_recv()
+
+    def compute(zo):
+        base = zo * nx
+        xs = X[pl.ds(base, nx)].reshape(nx * rows, X.shape[2])
+        xin = xs[:, :width]
+        O[...] = jnp.zeros_like(O)
+        for hh in range(2):
+            hid = silu_mul(jnp.dot(xin, Wg[hh], preferred_element_type=jnp.float32),
+                           jnp.dot(xin, Wu[hh], preferred_element_type=jnp.float32))
+            O[...] += jnp.dot(hid, Wd[hh], preferred_element_type=jnp.float32)
+        lo = width // 128 * 128
+        tail = xs[:, lo:].astype(jnp.float32)
+        lane = lax.broadcasted_iota(jnp.int32, tail.shape, 1) - (width - lo)
+        n_all = nz * nx
+        hit = (lane == me) | (lane == me + n_all) | (lane == me + 2 * n_all)
+        weight = jnp.sum(jnp.where(hit, tail, 0.0), axis=1, keepdims=True)
+        O[...] = weight * O[...].astype(jnp.bfloat16).astype(jnp.float32)
+        OWN[zo] = O[pl.ds(pl.multiple_of(x * rows, rows), rows), :]
+        PXs[zo] = O[pl.ds(pl.multiple_of(ox * rows, rows), rows), :].astype(jnp.bfloat16)
+
+    def column_sum(zo):
+        p_copy(zo).wait_recv()
+        CSs[zo] = (OWN[zo] + PXr[zo].astype(jnp.float32)).astype(jnp.bfloat16)
+        c_copy(zo, z).start()
+
+    for i in range(nz):
+        zi = nth(i)
+        if i + 1 < nz:
+            zn = nth(i + 1)
+            z_copy(zn, 0).wait_recv()
+            forward(zn)
+        if i >= 3:
+            column_sum(nth(i - 2))
+        x_copy(zi, ox).wait_recv()
+        compute(zi)
+        if i > 0:
+            p_copy(zi).start()
+    p_copy(z).start()
+    for i in range(max(1, nz - 2), nz):
+        column_sum(nth(i))
+    p_copy(z).wait_recv()
+    OWN[z] += PXr[z].astype(jnp.float32)
+    for i in range(1, nz):
+        zi = nth(i)
+        c_copy(zi, zi).wait_recv()
+        OWN[z] += CSr[zi].astype(jnp.float32)
+
+    @pl.when(core == 0)
+    def _():
+        FXs[...] = OWN[z, :, half:]
+
+    @pl.when(core == 1)
+    def _():
+        FXs[...] = OWN[z, :, :half]
+    fx_copy = remote(FXs, FXr, m_send.at[1], m_recv.at[1], tensor=1 - core)
+    fx_copy.start()
+    sh_copy.wait_recv()
+    fx_copy.wait_recv()
+
+    for cc in range(2):
+        @pl.when(core == cc)
+        def _():
+            cols = slice(cc * half, (cc + 1) * half)
+            for hh in range(2):
+                rr = slice(hh * rows, (hh + 1) * rows)
+                routed = OWN[z, :, cols] if hh == cc else FXr[...]
+                total = tok_ref[rr, cols].astype(jnp.float32) + routed + (SHo[rr, cols] + SHr[rr, :])
+                out_ref[rr, :] = total.astype(jnp.bfloat16)
+
+    for cp in rem_w:
+        cp.wait_send()
+    sh_copy.wait_send()
+    fx_copy.wait_send()
+    for i in range(nz):
+        zo = i
+
+        @pl.when(jnp.logical_and(zo <= z, z + 1 < nz))
+        def _():
+            z_copy(zo, 0).wait_send()
+
+        @pl.when(jnp.logical_and(zo >= z, z >= 1))
+        def _():
+            z_copy(zo, 1).wait_send()
+
+        x_copy(zo, x).wait_send()
+        p_copy(zo).wait_send()
+
+        @pl.when(zo != z)
+        def _():
+            c_copy(zo, z).wait_send()
+
+
+def pad(n, m):
+    return -(-n // m) * m
+
+
+def gather_plan(tok_count, width, expert_count, local_experts, hidden):
+    if local_experts != 1 or expert_count % 2 or tok_count % 32 or width % 2:
+        return None
+    nz, rows = expert_count // 2, tok_count // 2
+    ext = pad(width + 3 * expert_count, 128)
+    if ext - width // 128 * 128 > 128:
+        return None
+    wide, hid, half = pad(width, 128), pad(hidden, 128), pad(width // 2, 128)
+    weights = 9 * (2 * width * hid + pad(hidden, 16) * wide) * 2 // 3 + 0
+    moved = expert_count * rows * ext * 2 + 4 * nz * rows * wide * 2 + nz * rows * wide * 4
+    flat = tok_count * (2 * wide * 4 + 2 * half * 4 + 2 * wide * 2) + 2 * rows * half * 4
+    return weights + moved + flat
+
+
+def gather_local(tokens, routes, gates, w_gate, w_up, w_down, shared_gate, shared_up, shared_down):
+    tok_count, width = tokens.shape
+    hidden = w_gate.shape[2]
+    n = lax.axis_size("expert")
+    nx, nz = 2, n // 2
+    rows, half = tok_count // 2, width // 2
+    ext_w = pad(width + 3 * n, 128)
+    core = lax.axis_index("tensor")
+    first = core * rows
+    toks = lax.dynamic_slice_in_dim(tokens, first, rows, 0)
+    rts = lax.dynamic_slice_in_dim(routes, first, rows, 0)
+    gts = lax.dynamic_slice_in_dim(gates, first, rows, 0)
+    named = rts[:, :, None] == jnp.arange(n, dtype=jnp.int32)[None, None, :]
+    dense = jnp.sum(jnp.where(named, gts[:, :, None], 0.0), axis=1)
+    hi = lax.reduce_precision(dense, 8, 7)
+    mid = lax.reduce_precision(dense - hi, 8, 7)
+    low = dense - hi - mid
+    terms = jnp.concatenate([hi, mid, low, jnp.zeros((rows, ext_w - width - 3 * n), jnp.float32)], 1)
+    ext = jnp.concatenate([toks, terms.astype(jnp.bfloat16)], 1)
+    bf, f32 = jnp.bfloat16, jnp.float32
+    vm, dma = pltpu.VMEM, pltpu.SemaphoreType.DMA
+    scratch = [
+        vm((n, rows, ext_w), bf),
+        vm((2, width, hidden), bf), vm((2, width, hidden), bf), vm((2, hidden, width), bf),
+        vm((width, hidden), bf), vm((width, hidden), bf), vm((hidden, width), bf),
+        vm((nz, rows, width), f32), vm((nx * rows, width), f32),
+        vm((nz, rows, width), bf), vm((nz, rows, width), bf), vm((nz, rows, width), bf), vm((nz, rows, width), bf),
+        vm((tok_count, width), f32), vm((tok_count, half), f32), vm((tok_count, half), f32),
+        vm((rows, half), f32), vm((rows, half), f32),
+        dma((3,)), dma((3,)), dma((3,)), dma((3,)), dma((2, nz)), dma((nz,)), dma((nz,)), dma((nz,)),
+        dma((nz,)), dma((nz,)), dma((nz,)), dma((nz,)), dma((2,)), dma((2,)),
+    ]
+    in_vmem, in_hbm = pl.BlockSpec(memory_space=pltpu.VMEM), pl.BlockSpec(memory_space=pl.ANY)
+    return pl.pallas_call(
+        functools.partial(moe_kernel, nz, nx, width),
+        out_shape=jax.ShapeDtypeStruct((tok_count, half), bf),
+        in_specs=[in_vmem] * 2 + [in_hbm] * 6,
+        out_specs=in_vmem,
+        scratch_shapes=scratch,
+        compiler_params=pltpu.CompilerParams(collective_id=0, has_side_effects=True, vmem_limit_bytes=60 * 1024 * 1024),
+    )(ext, tokens, w_gate, w_up, w_down, shared_gate, shared_up, shared_down)
+
+
+def local(tokens, routes, gates, w_gate, *rest):
+    need = gather_plan(*tokens.shape, lax.axis_size("expert"), w_gate.shape[0], w_gate.shape[2])
+    if need is not None and lax.axis_size("tensor") == 2 and need <= VMEM_BUDGET:
+        return gather_local(tokens, routes, gates, w_gate, *rest)
+    return exchange_local(tokens, routes, gates, w_gate, *rest)
 
 
 def solution(mesh):

time: 277 us -> 104 us (0.38)
  the two profiles are of different devices: /device:TPU:1 before, /device:TPU:25 now
where the time goes in v1:
time: 104 us
  Pallas kernels  98.1 us (94%)
  local copies, waits for them, and re-layouts  5.98 us (6%)
    pallas_call x1, Pallas kernels, gather_local(): pl.pallas_call(functools.partial(moe_kernel, nz, nx, width), out_shape=ja...  98.1 us
    unnamed x5, local copies, waits for them, and re-layouts  2.08 us

profile of v1, /device:TPU:25, one launch (start us, length us, event | category | flops | bytes accessed | tf_op | source)
XLA Modules:
  0.0 104.2 jit_solution(8931889099604577114)
XLA Ops:
  0.0 0.0 copy-start
  0.0 0.7 copy-done
  0.7 0.7 constant_dynamic-slice_fusion
  1.4 0.1 copy.23
  1.5 0.1 copy.22
  1.6 0.1 copy.21
  1.7 1.4 %copy.20.tok_ref = bf16[256,1440]{1,0:T(8,128)(2,1)S(1)} copy(bf16[256,1440]{0,1:T(8,128)(2,1)} %param.9) | data formatting | bytes 1474560 | tf_op args[0]
  3.1 0.0 copy-start.1
  3.2 0.9 concatenate.6.ext_ref
  4.1 0.0 copy-done.1
  4.1 98.1 %shard_map.91 = bf16[256,720]{1,0:T(8,128)(2,1)} custom-call(bf16[128,1536]{1,0:T(8,128)(2,1)} %concatenate.6.ext_ref, bf16[256,1440]{1,0:T(8,128)(2,1)} %copy-done.1, bf16[1,1440,720]{2,1,0:T(8,128)(2,1)} %wg_ref.1, bf16[1,1440,720]{2,1,0:T(8,128)(2,1)} %wu_ref.1, bf16[1,720,1440]{2,1,0:T(8,128)(2,1)} %wd_ref.1, bf16[1440,720]{1,0:T(8,128)(2,1)} %sg_ref.1, ...), custom_call_target="tpu_custom_call" | custom-call | tf_op jit(solution)/shard_map/pallas_call | solution.py:303
  102.3 1.9 %copy.25 = bf16[256,720]{0,1:T(8,128)(2,1)} copy(bf16[256,720]{1,0:T(8,128)(2,1)} %shard_map.91) | data formatting | bytes 737280 | tf_op jit(solution)/shard_map/pallas_call | solution.py:303
  (6 shorter events, 0.1 us)
Async XLA Ops:
  0.0 0.7 copy-start
  3.1 1.0 copy-start.1

commit v2 on v1

--- a/solution.py
+++ b/solution.py
@@ -63,7 +63,7 @@
     return (g / (1.0 + jnp.exp(-g)) * u).astype(jnp.bfloat16)
 
 
-def moe_kernel(nz, nx, width, ext_ref, tok_ref, wg_ref, wu_ref, wd_ref, sg_ref, su_ref, sd_ref, out_ref,
+def moe_kernel(nz, nx, width, tok_ref, routes_ref, gates_ref, wg_ref, wu_ref, wd_ref, sg_ref, su_ref, sd_ref, out_ref,
                X, Wg, Wu, Wd, Sg, Su, Sd, OWN, O, PXs, PXr, CSs, CSr, SHo, SHs, SHr, FXs, FXr,
                w_loc, s_loc, w_send, w_recv, z_send, z_recv, x_send, x_recv, p_send, p_recv,
                c_send, c_recv, m_send, m_recv):
@@ -73,7 +73,7 @@
     x = me % nx
     ox = nx - 1 - x
     other = z * nx + ox
-    rows = ext_ref.shape[0]
+    rows = tok_ref.shape[0] // 2
     half = out_ref.shape[1]
 
     barrier = pltpu.get_barrier_semaphore()
@@ -89,7 +89,24 @@
         ((wg_ref, Wg), (wu_ref, Wu), (wd_ref, Wd)))]
     for cp in loc_s + loc_w:
         cp.start()
-    X[me] = ext_ref[...]
+    n_all = nz * nx
+    lo = width // 128 * 128
+    spare = X.shape[2] - lo
+
+    def own_half(ref):
+        return jnp.where(core == 0, ref[:, :rows], ref[:, rows:])
+    named, gate = own_half(routes_ref), own_half(gates_ref)
+    slot = lax.broadcasted_iota(jnp.int32, (spare, rows), 0) - (width - lo)
+    dense = jnp.zeros((spare, rows), jnp.float32)
+    for k in range(named.shape[0]):
+        for term in range(3):
+            dense = jnp.where(slot - term * n_all == named[k:k + 1, :], gate[k:k + 1, :], dense)
+    hi = dense.astype(jnp.bfloat16).astype(jnp.float32)
+    mid = (dense - hi).astype(jnp.bfloat16).astype(jnp.float32)
+    low = dense - hi - mid
+    terms = jnp.where(slot < n_all, hi, jnp.where(slot < 2 * n_all, mid, low))
+    X[me, :, lo:] = terms.T.astype(jnp.bfloat16)
+    X[me, :, :width] = tok_ref[pl.ds(pl.multiple_of(core * rows, rows), rows), :]
     pl.semaphore_wait(barrier, nz + 1)
 
     def remote(src, dst, ssem, rsem, **dev):
@@ -105,7 +122,7 @@
         e = zo * nx + col
         return remote(X.at[e], X.at[e], x_send.at[zo], x_recv.at[zo], expert=other)
 
-    def forward(zo):
+    def forward_z(zo):
         @pl.when(jnp.logical_and(zo <= z, z + 1 < nz))
         def _():
             z_copy(zo, 0).start()
@@ -114,7 +131,12 @@
         def _():
             z_copy(zo, 1).start()
 
+    def forward_x(zo):
         x_copy(zo, x).start()
+
+    def take_z(zo):
+        z_copy(zo, 0).wait_recv()
+        forward_z(zo)
 
     def p_copy(zo):
         return remote(PXs.at[zo], PXr.at[zo], p_send.at[zo], p_recv.at[zo], expert=other)
@@ -122,13 +144,14 @@
     def c_copy(zo, slot):
         return remote(CSs.at[zo], CSr.at[slot], c_send.at[zo], c_recv.at[slot], expert=zo * nx + x)
 
-    forward(z)
+    forward_z(z)
+    forward_x(z)
     rem_w = [remote(a.at[0], b.at[1], w_send.at[i], w_recv.at[i], tensor=1 - core) for i, (a, b) in enumerate(
         ((wg_ref, Wg), (wu_ref, Wu), (wd_ref, Wd)))]
     for cp in rem_w:
         cp.start()
 
-    table = [sorted(range(nz), key=lambda q: (abs(q - k), q)) for k in range(nz)]
+    table = [sorted(range(nz), key=lambda q: (abs(q - k), abs(2 * q + 1 - nz))) for k in range(nz)]
 
     def nth(i):
         r = table[0][i]
@@ -167,10 +190,8 @@
             hid = silu_mul(jnp.dot(xin, Wg[hh], preferred_element_type=jnp.float32),
                            jnp.dot(xin, Wu[hh], preferred_element_type=jnp.float32))
             O[...] += jnp.dot(hid, Wd[hh], preferred_element_type=jnp.float32)
-        lo = width // 128 * 128
         tail = xs[:, lo:].astype(jnp.float32)
         lane = lax.broadcasted_iota(jnp.int32, tail.shape, 1) - (width - lo)
-        n_all = nz * nx
         hit = (lane == me) | (lane == me + n_all) | (lane == me + 2 * n_all)
         weight = jnp.sum(jnp.where(hit, tail, 0.0), axis=1, keepdims=True)
         O[...] = weight * O[...].astype(jnp.bfloat16).astype(jnp.float32)
@@ -184,10 +205,24 @@
 
     for i in range(nz):
         zi = nth(i)
-        if i + 1 < nz:
-            zn = nth(i + 1)
-            z_copy(zn, 0).wait_recv()
-            forward(zn)
+
+        @pl.when(jnp.logical_or(z == 0, z == nz - 1))
+        def _():
+            if i + 1 < nz:
+                take_z(nth(i + 1))
+                forward_x(nth(i + 1))
+
+        @pl.when(jnp.logical_and(z > 0, z < nz - 1))
+        def _():
+            if i == 0:
+                for j in range(1, min(3, nz)):
+                    take_z(nth(j))
+                    forward_x(nth(j))
+            else:
+                if i + 2 < nz:
+                    take_z(nth(i + 2))
+                if 2 <= i < nz - 1:
+                    forward_x(nth(i + 1))
         if i >= 3:
             column_sum(nth(i - 2))
         x_copy(zi, ox).wait_recv()
@@ -274,18 +309,6 @@
     nx, nz = 2, n // 2
     rows, half = tok_count // 2, width // 2
     ext_w = pad(width + 3 * n, 128)
-    core = lax.axis_index("tensor")
-    first = core * rows
-    toks = lax.dynamic_slice_in_dim(tokens, first, rows, 0)
-    rts = lax.dynamic_slice_in_dim(routes, first, rows, 0)
-    gts = lax.dynamic_slice_in_dim(gates, first, rows, 0)
-    named = rts[:, :, None] == jnp.arange(n, dtype=jnp.int32)[None, None, :]
-    dense = jnp.sum(jnp.where(named, gts[:, :, None], 0.0), axis=1)
-    hi = lax.reduce_precision(dense, 8, 7)
-    mid = lax.reduce_precision(dense - hi, 8, 7)
-    low = dense - hi - mid
-    terms = jnp.concatenate([hi, mid, low, jnp.zeros((rows, ext_w - width - 3 * n), jnp.float32)], 1)
-    ext = jnp.concatenate([toks, terms.astype(jnp.bfloat16)], 1)
     bf, f32 = jnp.bfloat16, jnp.float32
     vm, dma = pltpu.VMEM, pltpu.SemaphoreType.DMA
     scratch = [
@@ -303,11 +326,11 @@
     return pl.pallas_call(
         functools.partial(moe_kernel, nz, nx, width),
         out_shape=jax.ShapeDtypeStruct((tok_count, half), bf),
-        in_specs=[in_vmem] * 2 + [in_hbm] * 6,
+        in_specs=[in_vmem] * 3 + [in_hbm] * 6,
         out_specs=in_vmem,
         scratch_shapes=scratch,
         compiler_params=pltpu.CompilerParams(collective_id=0, has_side_effects=True, vmem_limit_bytes=60 * 1024 * 1024),
-    )(ext, tokens, w_gate, w_up, w_down, shared_gate, shared_up, shared_down)
+    )(tokens, routes.T, gates.T, w_gate, w_up, w_down, shared_gate, shared_up, shared_down)
 
 
 def local(tokens, routes, gates, w_gate, *rest):

time: 104 us -> 97.8 us (0.940)
  the two profiles are of different devices: /device:TPU:25 before, /device:TPU:1 now
where the time goes in v2:
time: 97.8 us; the launch traced here: 97.5 us
  Pallas kernels  93.4 us (96%)
  local copies, waits for them, and re-layouts  4.17 us (4%)
    pallas_call x1, Pallas kernels, gather_local(): pl.pallas_call(functools.partial(moe_kernel, nz, nx, width), out_shape=ja...  93.4 us
    unnamed x1, local copies, waits for them, and re-layouts  2.27 us

profile of v2, /device:TPU:1, one launch (start us, length us, event | category | flops | bytes accessed | tf_op | source)
XLA Modules:
  0.0 97.5 jit_solution(7944941463835922299)
XLA Ops:
  0.0 2.3 %copy.10.tok_ref = bf16[256,1440]{1,0:T(8,128)(2,1)} copy(bf16[256,1440]{0,1:T(8,128)(2,1)} %param.9) | data formatting | bytes 1474560 | tf_op args[0]
  2.3 93.4 %shard_map.91 = bf16[256,720]{1,0:T(8,128)(2,1)} custom-call(bf16[256,1440]{1,0:T(8,128)(2,1)} %copy.10.tok_ref, s32[4,256]{1,0:T(4,128)} %bitcast.2, f32[4,256]{1,0:T(4,128)} %bitcast.3, bf16[1,1440,720]{2,1,0:T(8,128)(2,1)} %wg_ref.1, bf16[1,1440,720]{2,1,0:T(8,128)(2,1)} %wu_ref.1, bf16[1,720,1440]{2,1,0:T(8,128)(2,1)} %wd_ref.1, ...), custom_call_target="tpu_custom_call" | custom-call | tf_op jit(solution)/shard_map/pallas_call | solution.py:326
  95.6 1.9 %copy.11 = bf16[256,720]{0,1:T(8,128)(2,1)} copy(bf16[256,720]{1,0:T(8,128)(2,1)} %shard_map.91) | data formatting | bytes 737280 | tf_op jit(solution)/shard_map/pallas_call | solution.py:326

commit v3 on v2

--- a/solution.py
+++ b/solution.py
@@ -138,11 +138,15 @@
         z_copy(zo, 0).wait_recv()
         forward_z(zo)
 
-    def p_copy(zo):
-        return remote(PXs.at[zo], PXr.at[zo], p_send.at[zo], p_recv.at[zo], expert=other)
-
-    def c_copy(zo, slot):
-        return remote(CSs.at[zo], CSr.at[slot], c_send.at[zo], c_recv.at[slot], expert=zo * nx + x)
+    part = rows // 2
+
+    def p_copy(zo, h):
+        r = pl.ds(h * part, part)
+        return remote(PXs.at[zo, r], PXr.at[zo, r], p_send.at[h, zo], p_recv.at[h, zo], expert=other)
+
+    def c_copy(zo, slot, h):
+        r = pl.ds(h * part, part)
+        return remote(CSs.at[zo, r], CSr.at[slot, r], c_send.at[h, zo], c_recv.at[h, slot], expert=zo * nx + x)
 
     forward_z(z)
     forward_x(z)
@@ -199,9 +203,11 @@
         PXs[zo] = O[pl.ds(pl.multiple_of(ox * rows, rows), rows), :].astype(jnp.bfloat16)
 
     def column_sum(zo):
-        p_copy(zo).wait_recv()
-        CSs[zo] = (OWN[zo] + PXr[zo].astype(jnp.float32)).astype(jnp.bfloat16)
-        c_copy(zo, z).start()
+        for h in range(2):
+            r = slice(h * part, (h + 1) * part)
+            p_copy(zo, h).wait_recv()
+            CSs[zo, r] = (OWN[zo, r] + PXr[zo, r].astype(jnp.float32)).astype(jnp.bfloat16)
+            c_copy(zo, z, h).start()
 
     for i in range(nz):
         zi = nth(i)
@@ -228,15 +234,19 @@
         x_copy(zi, ox).wait_recv()
         compute(zi)
         if i > 0:
-            p_copy(zi).start()
-    p_copy(z).start()
+            for h in range(2):
+                p_copy(zi, h).start()
+    for h in range(2):
+        p_copy(z, h).start()
     for i in range(max(1, nz - 2), nz):
         column_sum(nth(i))
-    p_copy(z).wait_recv()
+    for h in range(2):
+        p_copy(z, h).wait_recv()
     OWN[z] += PXr[z].astype(jnp.float32)
     for i in range(1, nz):
         zi = nth(i)
-        c_copy(zi, zi).wait_recv()
+        for h in range(2):
+            c_copy(zi, zi, h).wait_recv()
         OWN[z] += CSr[zi].astype(jnp.float32)
 
     @pl.when(core == 0)
@@ -277,11 +287,13 @@
             z_copy(zo, 1).wait_send()
 
         x_copy(zo, x).wait_send()
-        p_copy(zo).wait_send()
+        for h in range(2):
+            p_copy(zo, h).wait_send()
 
         @pl.when(zo != z)
         def _():
-            c_copy(zo, z).wait_send()
+            for h in range(2):
+                c_copy(zo, z, h).wait_send()
 
 
 def pad(n, m):
@@ -320,7 +332,7 @@
         vm((tok_count, width), f32), vm((tok_count, half), f32), vm((tok_count, half), f32),
         vm((rows, half), f32), vm((rows, half), f32),
         dma((3,)), dma((3,)), dma((3,)), dma((3,)), dma((2, nz)), dma((nz,)), dma((nz,)), dma((nz,)),
-        dma((nz,)), dma((nz,)), dma((nz,)), dma((nz,)), dma((2,)), dma((2,)),
+        dma((2, nz)), dma((2, nz)), dma((2, nz)), dma((2, nz)), dma((2,)), dma((2,)),
     ]
     in_vmem, in_hbm = pl.BlockSpec(memory_space=pltpu.VMEM), pl.BlockSpec(memory_space=pl.ANY)
     return pl.pallas_call(

time: 97.8 us -> 93.7 us (0.958)
  Pallas kernels: 93.4 us -> 89.3 us
    pallas_call x1, Pallas kernels: 93.4 us -> 89.3 us  [gather_local(): pl.pallas_call(functools.partial(moe_kernel, nz, nx, width), out_shape=ja...]
where the time goes in v3:
time: 93.7 us; the launch traced here: 93.4 us
  Pallas kernels  89.3 us (95%)
  local copies, waits for them, and re-layouts  4.17 us (4%)
    pallas_call x1, Pallas kernels, gather_local(): pl.pallas_call(functools.partial(moe_kernel, nz, nx, width), out_shape=ja...  89.3 us
    unnamed x1, local copies, waits for them, and re-layouts  2.27 us
    pallas_call x1, local copies, waits for them, and re-layouts, gather_local(): pl.pallas_call(functools.partial(moe_kernel, nz, nx, width), out_shape=ja...  1.91 us

profile of v3, /device:TPU:1, one launch (start us, length us, event | category | flops | bytes accessed | tf_op | source)
XLA Modules:
  0.0 93.4 jit_solution(2385855431023868433)
XLA Ops:
  0.0 2.3 %copy.10.tok_ref = bf16[256,1440]{1,0:T(8,128)(2,1)} copy(bf16[256,1440]{0,1:T(8,128)(2,1)} %param.9) | data formatting | bytes 1474560 | tf_op args[0]
  2.3 89.3 %shard_map.91 = bf16[256,720]{1,0:T(8,128)(2,1)} custom-call(bf16[256,1440]{1,0:T(8,128)(2,1)} %copy.10.tok_ref, s32[4,256]{1,0:T(4,128)} %bitcast.2, f32[4,256]{1,0:T(4,128)} %bitcast.3, bf16[1,1440,720]{2,1,0:T(8,128)(2,1)} %wg_ref.1, bf16[1,1440,720]{2,1,0:T(8,128)(2,1)} %wu_ref.1, bf16[1,720,1440]{2,1,0:T(8,128)(2,1)} %wd_ref.1, ...), custom_call_target="tpu_custom_call" | custom-call | tf_op jit(solution)/shard_map/pallas_call | solution.py:338
  91.5 1.9 %copy.11 = bf16[256,720]{0,1:T(8,128)(2,1)} copy(bf16[256,720]{1,0:T(8,128)(2,1)} %shard_map.91) | data formatting | bytes 737280 | tf_op jit(solution)/shard_map/pallas_call | solution.py:338
